TPU v7x, 32 devices: a whole 2x2x4 slice. The times are simulated.
32 devices in a mesh: gx: 4 (over z), gy: 2 (over y), gz: 4 (over x, core).
Axes of the slice: x: 2, y: 2, z: 4, core: 2. Of those that a mesh axis runs over, the one named last changes fastest.
Arguments:
- displacement: float32 [3, 64, 64, 1024], P(None, 'gx', 'gy', 'gz'), may hold values from -1.5 to 1.5
- density: float32 [64, 64, 1024], P('gx', 'gy', 'gz'), may hold values from 0.03 to 1
- stiffness: float32 [24, 24], replicated, may hold values from -9 to 9.5, as said below
Outputs:
- filtered: float32 [64, 64, 1024], P('gx', 'gy', 'gz')
- compliance: float32 [], replicated
- volume: float32 [], replicated
Inputs may be any that keep to these rules, and one draw needn't show every extreme that they name: `stiffness`: symmetric and positive definite, every eigenvalue at least 0.5.
All inputs are finite; a program needn't handle non-finite values.
Results may differ from a plain program's by a relative error of at most 0.00005.
Values sent between devices are 32-bit elements; how exact they have to be, the bound alone decides.
A program may use at most 64 MiB of HBM per device.

v0:
```python
import jax
import jax.numpy as jnp
from jax import lax
from jax.sharding import PartitionSpec as P

VOID_STIFFNESS = 0.001
KERNEL = (1.0, 2.0, 3.0, 2.0, 1.0)


def from_behind(block, axis, distance):
    devices = range(lax.axis_size(axis))
    route = [(i - distance, i) for i in devices if i - distance in devices]
    return lax.ppermute(block, axis, route)


def with_halo(shard, sides, width):
    for axis, dim in sides:
        count, length = (lax.axis_size(axis), shard.shape[dim])
        up = [(i, (i + 1) % count) for i in range(count - 1)]
        down = [(j, i) for i, j in up]
        last = lax.slice_in_dim(shard, length - width, length, axis=dim)
        first = lax.slice_in_dim(shard, 0, width, axis=dim)
        before = lax.ppermute(last, axis, up)
        after = lax.ppermute(first, axis, down)
        shard = jnp.concatenate([before, shard, after], axis=dim)
    return shard


def smooth(values, along):
    length = values.shape[along] - 4
    summed = None
    for offset in range(5):
        section = lax.slice_in_dim(values, offset, offset + length, axis=along)
        scaled = KERNEL[offset] * section
        summed = scaled if summed is None else summed + scaled
    return summed


def side_sums(first, amount, extent):
    position = first + jnp.arange(amount, dtype=jnp.int32)
    summed = jnp.zeros((amount,), jnp.float32)
    for offset in range(5):
        inside = (position + offset - 2 >= 0) & (position + offset - 2 < extent)
        summed = summed + KERNEL[offset] * inside.astype(jnp.float32)
    return summed


def plane_energy(slab_nodes, stiffness):
    height = slab_nodes.shape[2] - 1
    length = slab_nodes.shape[3] - 1
    corner_rows = jnp.stack(
        [
            slab_nodes[
                member, along_x, along_y : along_y + height, along_z : along_z + length
            ].reshape(-1)
            for member in range(3)
            for along_x in range(2)
            for along_y in range(2)
            for along_z in range(2)
        ]
    )
    product = jnp.dot(
        stiffness, corner_rows, precision=lax.Precision.HIGHEST, preferred_element_type=jnp.float32
    )
    return jnp.sum(corner_rows * product, axis=0).reshape(height, length)


def energies(node_field, stiffness, planes):

    def one_plane(plane_index):
        slab_nodes = lax.dynamic_slice_in_dim(node_field, plane_index, 2, 1)
        return plane_energy(slab_nodes, stiffness)

    return lax.map(one_plane, jnp.arange(planes, dtype=jnp.int32))


def hole_sums(cells_first, cells_second, cells_third, margin):
    first_sums = side_sums(
        lax.axis_index("gx") * cells_first - margin,
        cells_first + 2 * margin,
        cells_first * lax.axis_size("gx"),
    )
    second_sums = side_sums(
        lax.axis_index("gy") * cells_second - margin,
        cells_second + 2 * margin,
        cells_second * lax.axis_size("gy"),
    )
    third_sums = side_sums(
        lax.axis_index("gz") * cells_third - margin,
        cells_third + 2 * margin,
        cells_third * lax.axis_size("gz"),
    )
    return first_sums[:, None, None] * second_sums[None, :, None] * third_sums[None, None, :]


def on_device(displacement, density, stiffness):
    cells_first, cells_second, cells_third = density.shape
    modulus = VOID_STIFFNESS + density * density * density * (1.0 - VOID_STIFFNESS)
    node_field = displacement
    upper_layer = from_behind(node_field[:, :1], "gx", -1)
    node_field = jnp.concatenate([node_field, upper_layer], axis=1)
    upper_layer = from_behind(node_field[:, :, :1], "gy", -1)
    node_field = jnp.concatenate([node_field, upper_layer], axis=2)
    upper_layer = from_behind(node_field[:, :, :, :1], "gz", -1)
    node_field = jnp.concatenate([node_field, upper_layer], axis=3)
    energy = energies(node_field, stiffness, cells_first)
    sensitivity = -3.0 * (1.0 - VOID_STIFFNESS) * density * density * energy
    weighted = sensitivity / hole_sums(cells_first, cells_second, cells_third, 0)
    spread = with_halo(weighted, (("gx", 0), ("gy", 1), ("gz", 2)), 2)
    filtered = smooth(smooth(smooth(spread, 0), 1), 2)
    totals = lax.psum((jnp.sum(modulus * energy), jnp.sum(density)), ("gx", "gy", "gz"))
    cell_count = float(
        cells_first
        * cells_second
        * cells_third
        * lax.axis_size("gx")
        * lax.axis_size("gy")
        * lax.axis_size("gz")
    )
    return (filtered, totals[0] / cell_count, totals[1] / cell_count)


def solution(mesh):
    return jax.shard_map(
        on_device,
        mesh=mesh,
        in_specs=(P(None, "gx", "gy", "gz"), P("gx", "gy", "gz"), P()),
        out_specs=(P("gx", "gy", "gz"), P(), P()),
        check_vma=False,
    )
```

profile of v0, /device:TPU:0, one launch (start us, length us, event | category | flops | bytes accessed | tf_op | source)
XLA Modules:
  0.0 206.7 jit_solution(15581065391671610939)
XLA Ops:
  0.6 0.9 slice.144
  1.5 1.3 collective-permute-start
  2.8 1.5 constant_dynamic-update-slice_fusion.2
  4.4 4.9 %collective-permute-done = f32[3,1,32,256]{3,2,1,0:T(8,128)S(1)} collective-permute-done((f32[3,1,32,256]{3,2,1,0:T(8,128)S(1)}, f32[3,1,32,256]{3,2,1,0:T(8,128)S(1)}, u32[]{:S(2)}, u32[]{:S(2)}) %collective-permute-start) | collective-permute-done | bytes 98336 | tf_op jit(solution)/shard_map/ppermute | solution.py:13
  9.3 1.3 collective-permute-start.1
  10.7 4.6 %collective-permute-done.1 = f32[3,17,1,256]{3,2,1,0:T(1,128)S(1)} collective-permute-done((f32[3,17,1,256]{3,2,1,0:T(1,128)S(1)}, f32[3,17,1,256]{3,2,1,0:T(1,128)S(1)}, u32[]{:S(2)}, u32[]{:S(2)}) %collective-permute-start.1) | collective-permute-done | bytes 52256 | tf_op jit(solution)/shard_map/ppermute | solution.py:13
  15.9 1.3 collective-permute-start.2
  17.2 1.8 collective-permute-done.2
  19.5 1.9 pad_maximum_fusion
  21.4 115.6 %while.10 = (s32[]{:T(128)}, f32[16,32,256]{2,1,0:T(8,128)S(1)}, s32[16]{0:T(128)S(1)}, f32[3,17,33,257]{3,2,1,0:T(8,128)}, f32[24,24]{1,0:T(8,128)S(1)}, /*index=5*/s32[]{:T(128)}, s32[]{:T(128)}, s32[]{}, s32[]{:T(128)}, s32[]{}) while((s32[]{:T(128)}, f32[16,32,256]{2,1,0:T(8,128)S(1)}, s32[16]{0:T(128)S(1)}, f32[3,17,33,257]{3,2,1,0:T(8,128)}, ...), condition=%wide.region_2.3_spmd, body=%wide.region_0.2_spmd.sunk | while | flops 57008136 | bytes 5671371 | solution.py:74
  23.9 1.6 dynamic-slice_bitcast_fusion.25
  26.5 1.2 stack.4
  31.1 1.7 dynamic-slice_bitcast_fusion.25
  33.8 1.2 stack.4
  34.9 0.8 fusion.39
  38.3 1.6 dynamic-slice_bitcast_fusion.25
  41.0 1.2 stack.4
  42.2 0.8 fusion.39
  45.6 1.6 dynamic-slice_bitcast_fusion.25
  48.2 1.2 stack.4
  49.3 0.8 fusion.39
  52.7 1.5 dynamic-slice_bitcast_fusion.25
  55.3 1.2 stack.4
  59.9 1.5 dynamic-slice_bitcast_fusion.25
  62.4 1.2 stack.4
  63.6 0.8 fusion.39
  67.0 1.7 dynamic-slice_bitcast_fusion.25
  69.8 1.2 stack.4
  70.9 0.8 fusion.39
  74.3 1.6 dynamic-slice_bitcast_fusion.25
  77.0 1.2 stack.4
  81.6 1.6 dynamic-slice_bitcast_fusion.25
  84.2 1.2 stack.4
  85.4 0.8 fusion.39
  88.8 1.6 dynamic-slice_bitcast_fusion.25
  91.4 1.2 stack.4
  92.5 0.8 fusion.39
  96.0 1.6 dynamic-slice_bitcast_fusion.25
  98.6 1.2 stack.4
  103.2 1.6 dynamic-slice_bitcast_fusion.25
  105.8 1.2 stack.4
  107.0 0.8 fusion.39
  110.4 1.6 dynamic-slice_bitcast_fusion.25
  113.0 1.2 stack.4
  114.2 0.8 fusion.39
  117.6 1.7 dynamic-slice_bitcast_fusion.25
  120.4 1.2 stack.4
  121.6 0.8 fusion.39
  125.0 1.6 dynamic-slice_bitcast_fusion.25
  127.6 1.2 stack.4
  128.8 0.8 fusion.39
  132.2 1.7 dynamic-slice_bitcast_fusion.25
  134.9 1.2 stack.4
  136.1 0.8 fusion.39
  137.7 3.7 %collective-permute-start.3 = (f32[2,32,256]{2,1,0:T(8,128)S(1)}, f32[2,32,256]{2,1,0:T(8,128)S(1)}, u32[]{:S(2)}, u32[]{:S(2)}) collective-permute-start(f32[2,32,256]{2,1,0:T(8,128)S(1)} %get-tuple-element.79), channel_id=1, source_target_pairs={{0,8},{8,16},{16,24},{1,9},{9,17},{17,25},{2,10},{10,18},{18,26},{... | collective-permute-start | bytes 196616 | tf_op jit(solution)/shard_map/ppermute | solution.py:23
  141.5 1.3 collective-permute-start.4
  143.4 4.3 %collective-permute-done.4 = f32[2,32,256]{2,1,0:T(8,128)S(1)} collective-permute-done((f32[2,32,256]{2,1,0:T(8,128)S(1)}, f32[2,32,256]{2,1,0:T(8,128)S(1)}, u32[]{:S(2)}, u32[]{:S(2)}) %collective-permute-start.4) | collective-permute-done | bytes 65568 | tf_op jit(solution)/shard_map/ppermute | solution.py:24
  147.7 1.6 collective-permute-start.5
  149.3 1.3 collective-permute-start.6
  150.9 4.2 %collective-permute-done.6 = f32[20,2,256]{2,1,0:T(2,128)S(1)} collective-permute-done((f32[20,2,256]{2,1,0:T(2,128)S(1)}, f32[20,2,256]{2,1,0:T(2,128)S(1)}, u32[]{:S(2)}, u32[]{:S(2)}) %collective-permute-start.6) | collective-permute-done | bytes 40992 | tf_op jit(solution)/shard_map/ppermute | solution.py:24
  155.5 1.3 collective-permute-start.7
  156.8 1.3 collective-permute-start.8
  158.1 42.4 %all-reduce = (f32[]{:T(128)}, f32[]{:T(128)}) all-reduce(f32[]{:T(128)} %get-tuple-element.37, f32[]{:T(128)} %get-tuple-element.36), channel_id=1, replica_groups=mesh['gx'=4,'gy'=2,'gz'=4] {'gx','gy','gz'}, use_global_device_ids=true, to_apply=%region_4.5 | all-reduce | flops 2 | bytes 16 | tf_op jit(solution)/shard_map/psum | solution.py:111
  203.0 1.4 slice_add_fusion.2
  (463 shorter events, 31.0 us)
Async XLA Ops:
  1.5 7.7 %collective-permute-start = (f32[3,1,32,256]{3,2,1,0:T(8,128)S(1)}, f32[3,1,32,256]{3,2,1,0:T(8,128)S(1)}, u32[]{:S(2)}, u32[]{:S(2)}) collective-permute-start(f32[3,1,32,256]{3,2,1,0:T(8,128)S(1)} %slice.144), channel_id=1, source_target_pairs={{8,0},{16,8},{24,16},{9,1},{17,9},{25,17},{10,2},{18,10},{26,18},{... | collective-permute-start | bytes 294920 | tf_op jit(solution)/shard_map/ppermute | solution.py:13
  9.3 6.0 %collective-permute-start.1 = (f32[3,17,1,256]{3,2,1,0:T(1,128)S(1)}, f32[3,17,1,256]{3,2,1,0:T(1,128)S(1)}, u32[]{:S(2)}, u32[]{:S(2)}) collective-permute-start(f32[3,17,1,256]{3,2,1,0:T(1,128)S(1)} %slice.168), channel_id=1, source_target_pairs={{4,0},{5,1},{6,2},{7,3},{12,8},{13,9},{14,10},{15,11},{20,16},{21,... | collective-permute-start | bytes 156680 | tf_op jit(solution)/shard_map/ppermute | solution.py:13
  15.9 3.1 %collective-permute-start.2 = (f32[3,17,33,1]{2,3,1,0:T(1,128)S(1)}, f32[3,17,33,1]{2,3,1,0:T(1,128)S(1)}, u32[]{:S(2)}, u32[]{:S(2)}) collective-permute-start(f32[3,17,33,1]{2,3,1,0:T(1,128)S(1)} %copy.11), channel_id=1, source_target_pairs={{1,0},{2,1},{3,2},{5,4},{6,5},{7,6},{9,8},{10,9},{11,10},{13,12},{... | collective-permute-start | bytes 20204 | tf_op jit(solution)/shard_map/ppermute | solution.py:13
  19.5 1.9 copy-start.1
  21.4 115.6 %copy-start = (f32[16,32,256]{2,1,0:T(8,128)S(1)}, f32[16,32,256]{2,1,0:T(8,128)}, u32[]{:S(2)}) copy-start(f32[16,32,256]{2,1,0:T(8,128)} %param.6) | copy-start | bytes 1572868
  137.7 5.6 %collective-permute-start.3 = (f32[2,32,256]{2,1,0:T(8,128)S(1)}, f32[2,32,256]{2,1,0:T(8,128)S(1)}, u32[]{:S(2)}, u32[]{:S(2)}) collective-permute-start(f32[2,32,256]{2,1,0:T(8,128)S(1)} %get-tuple-element.79), channel_id=1, source_target_pairs={{0,8},{8,16},{16,24},{1,9},{9,17},{17,25},{2,10},{10,18},{18,26},{... | collective-permute-start | bytes 196616 | tf_op jit(solution)/shard_map/ppermute | solution.py:23
  141.5 6.2 %collective-permute-start.4 = (f32[2,32,256]{2,1,0:T(8,128)S(1)}, f32[2,32,256]{2,1,0:T(8,128)S(1)}, u32[]{:S(2)}, u32[]{:S(2)}) collective-permute-start(f32[2,32,256]{2,1,0:T(8,128)S(1)} %get-tuple-element.80), channel_id=1, source_target_pairs={{8,0},{16,8},{24,16},{9,1},{17,9},{25,17},{10,2},{18,10},{26,18},{... | collective-permute-start | bytes 196616 | tf_op jit(solution)/shard_map/ppermute | solution.py:24
  147.7 3.3 %collective-permute-start.5 = (f32[20,2,256]{2,1,0:T(2,128)S(1)}, f32[20,2,256]{2,1,0:T(2,128)S(1)}, u32[]{:S(2)}, u32[]{:S(2)}) collective-permute-start(f32[20,2,256]{2,1,0:T(2,128)S(1)} %get-tuple-element.77), channel_id=1, source_target_pairs={{0,4},{1,5},{2,6},{3,7},{8,12},{9,13},{10,14},{11,15},{16,20},{17,... | collective-permute-start | bytes 122888 | tf_op jit(solution)/shard_map/ppermute | solution.py:23
  149.3 5.9 %collective-permute-start.6 = (f32[20,2,256]{2,1,0:T(2,128)S(1)}, f32[20,2,256]{2,1,0:T(2,128)S(1)}, u32[]{:S(2)}, u32[]{:S(2)}) collective-permute-start(f32[20,2,256]{2,1,0:T(2,128)S(1)} %get-tuple-element.78), channel_id=1, source_target_pairs={{4,0},{5,1},{6,2},{7,3},{12,8},{13,9},{14,10},{15,11},{20,16},{21,... | collective-permute-start | bytes 122888 | tf_op jit(solution)/shard_map/ppermute | solution.py:24
  155.5 46.3 %collective-permute-start.7 = (f32[20,36,2]{2,1,0:T(8,128)S(1)}, f32[20,36,2]{2,1,0:T(8,128)S(1)}, u32[]{:S(2)}, u32[]{:S(2)}) collective-permute-start(f32[20,36,2]{2,1,0:T(8,128)S(1)} %get-tuple-element.75), channel_id=1, source_target_pairs={{0,1},{1,2},{2,3},{4,5},{5,6},{6,7},{8,9},{9,10},{10,11},{12,13},{... | collective-permute-start | bytes 17288 | tf_op jit(solution)/shard_map/ppermute | solution.py:23
  156.8 45.0 %collective-permute-start.8 = (f32[20,36,2]{2,1,0:T(8,128)S(1)}, f32[20,36,2]{2,1,0:T(8,128)S(1)}, u32[]{:S(2)}, u32[]{:S(2)}) collective-permute-start(f32[20,36,2]{2,1,0:T(8,128)S(1)} %get-tuple-element.76), channel_id=1, source_target_pairs={{1,0},{2,1},{3,2},{5,4},{6,5},{7,6},{9,8},{10,9},{11,10},{13,12},{... | collective-permute-start | bytes 17288 | tf_op jit(solution)/shard_map/ppermute | solution.py:24
where the time goes:
time: 209 us; the launch traced here: 207 us
  local copies, waits for them, and re-layouts  71 us (34%)
  blocking collectives  42.4 us (20%)
  loops' own time  35 us (17%)
  waiting for transfers between devices  20.8 us (10%)
  starting transfers between devices  14.4 us (7%)
  matrix products  13.2 us (6%)
  other arithmetic  5.63 us (3%)
  between operations  4.4 us (2%)
    psum x1, blocking collectives, on_device(): lax.psum((jnp.sum(modulus * energy), jnp.sum(density)), ('gx', 'gy', 'gz'))  42.4 us
    while x400, local copies, waits for them, and re-layouts  39.2 us
    another operation x1, loops' own time, energies(): return lax.map(one_plane, jnp.arange(planes, dtype=jnp.int32))  35 us
    another operation x16, local copies, waits for them, and re-layouts, plane_energy(): jnp.stack([slab_nodes[member, along_x, along_y:along_y + height, along_z:...  18.5 us
    dot_general x16, matrix products, plane_energy(): jnp.dot(stiffness, corner_rows, precision=lax.Precision.HIGHEST, preferre...  13.2 us
    ppermute x3, waiting for transfers between devices, from_behind(): return lax.ppermute(block, axis, route)  11.3 us
    dynamic_slice x16, local copies, waits for them, and re-layouts, energies(): return lax.map(one_plane, jnp.arange(planes, dtype=jnp.int32))  9.38 us
    ppermute x3, waiting for transfers between devices, with_halo(): after = lax.ppermute(first, axis, down)  8.52 us
  transfers between devices with their start and end apart: 9, of which 7 were waited for; matrix products, arithmetic and copies ran while one was open for 1% of the time, Pallas kernels for 0%

commit v1 on v0

v1 whole, which is shorter than its diff:
```python
import functools

import jax
import jax.numpy as jnp
from jax import lax
from jax.experimental import pallas as pl
from jax.experimental.pallas import tpu as pltpu
from jax.sharding import PartitionSpec as P

VOID = 0.001
H = (1.0, 2.0, 3.0, 2.0, 1.0)
MESH = pl.DeviceIdType.MESH
AXES = ("gx", "gy", "gz")
F32 = jnp.float32
BF16 = jnp.bfloat16
NODE_STEPS = [(a, b, c) for a in (0, 1) for b in (0, 1) for c in (0, 1) if a + b + c]


def iota(shape, dim):
    return lax.broadcasted_iota(jnp.int32, shape, dim)


def line_sum(position, extent):
    total = None
    for d in range(5):
        at = position + (d - 2)
        term = jnp.where((at >= 0) & (at < extent), H[d], 0.0).astype(F32)
        total = term if total is None else total + term
    return total


def band_weights(stiff):
    rows, cols = 192, 256
    pick = jnp.where((iota((rows, 24), 0) >> 3) == iota((rows, 24), 1), 1.0, 0.0).astype(F32)

    def column(shape):
        col = iota(shape, 1)
        a, g, s = col >> 7, (col >> 4) & 7, col & 7
        cm = jnp.where(g == 6, s, g)
        c = jnp.where(cm >= 3, 1, 0)
        m = cm - 3 * c
        valid = (g < 6) | ((g == 6) & (s < 6))
        return 8 * m + 4 * a + c, valid, jnp.where(g == 6, 8, s), (col >> 3) & 1

    total = None
    for b in (0, 1):
        q, valid, _, _ = column((24, cols))
        place = jnp.where((iota((24, cols), 0) == q + 2 * b) & valid, 1.0, 0.0).astype(F32)
        wide = jnp.dot(stiff, place, precision=lax.Precision.HIGHEST, preferred_element_type=F32)
        tall = jnp.dot(pick, wide, precision=lax.Precision.HIGHEST, preferred_element_type=F32)
        _, _, jj, _ = column((rows, cols))
        term = jnp.where(jj - (iota((rows, cols), 0) & 7) == b, tall, 0.0)
        total = term if total is None else total + term
    high = total.astype(BF16).astype(F32)
    _, _, _, lo_col = column((rows, cols))
    low = jnp.where(lo_col == 0, total - high, 0.0)
    return high.astype(BF16), low.astype(BF16)


def kernel(
    sizes, u, rho, stiff, out, comp, vol,
    rx, ry, rxy, rz, ys, zs, field, parts, weights, wx, wy, yslo, yshi, rylo, ryhi,
    zslo, zshi, rzlo, rzhi, sums, nsend, nrecv, fsend, frecv, gsend, grecv,
):
    ni, nj, nk = rho.shape
    n = dict(zip(AXES, sizes))
    me = {axis: lax.axis_index(axis) for axis in AXES}
    down = {axis: me[axis] > 0 for axis in AXES}
    up = {axis: me[axis] < n[axis] - 1 for axis in AXES}

    def moved(step, sign):
        ids, ok = {}, None
        for axis, s in zip(AXES, step):
            if s:
                ids[axis] = me[axis] + sign * s
                flag = up[axis] if sign > 0 else down[axis]
                ok = flag if ok is None else jnp.logical_and(ok, flag)
        return ids, ok

    barrier = pltpu.get_barrier_semaphore()
    for axis in AXES:
        for off in range(1, n[axis]):
            pl.semaphore_signal(
                barrier, inc=1, device_id={axis: lax.rem(me[axis] + off, n[axis])}, device_id_type=MESH
            )
    for step in NODE_STEPS:
        if sum(step) > 1:
            for sign in (1, -1):
                ids, ok = moved(step, sign)

                @pl.when(ok)
                def _():
                    pl.semaphore_signal(barrier, inc=1, device_id=ids, device_id_type=MESH)

    lane = iota((nj, 128), 1)
    for m in range(3):
        for i in range(ni):
            ys[m, i : i + 1, :] = u[m, i, 0:1, :]

    def pack(i, acc):
        for m in range(3):
            at = m * ni + i
            acc = jnp.where(lane == at, pltpu.roll(u[m, i, :, 0:128], at, 1), acc)
        return acc

    zs[...] = lax.fori_loop(0, ni, pack, jnp.zeros((nj, 128), F32))
    high, low = band_weights(stiff[...])
    weights[0:192, :] = high
    weights[192:384, :] = low

    peers = sum(n[axis] - 1 for axis in AXES)
    for step in NODE_STEPS:
        if sum(step) > 1:
            for sign in (1, -1):
                peers = peers + jnp.where(moved(step, sign)[1], 1, 0)
    pl.semaphore_wait(barrier, peers)

    node_copies = []
    for at, step in enumerate(NODE_STEPS):
        a, b, c = step
        if c:
            src, dst = zs, rz.at[a, b]
        elif b:
            src, dst = (ys.at[:, 0:8, :], rxy) if a else (ys, ry)
        else:
            src, dst = u.at[:, 0], rx
        ids, ok = moved(step, -1)
        copy = pltpu.make_async_remote_copy(
            src_ref=src, dst_ref=dst, send_sem=nsend.at[at], recv_sem=nrecv.at[at],
            device_id=ids, device_id_type=MESH,
        )
        node_copies.append((copy, ok, moved(step, 1)[1], dst))

        @pl.when(ok)
        def _():
            copy.start()

    for copy, _, has, dst in node_copies:

        @pl.when(has)
        def _():
            copy.wait_recv()

        @pl.when(jnp.logical_not(has))
        def _():
            dst[...] = jnp.zeros(dst.shape, F32)

    last = iota((nj, nk), 1) == nk - 1
    last8 = iota((8, nk), 1) == nk - 1

    def place(m, to, base, row, col, corner, at):
        field[0, m, to, 0:nj, :] = base
        moved_base = pltpu.roll(base, nk - 1, 1)
        side = pltpu.roll(col, 127 - at, 1)
        field[1, m, to, 0:nj, :] = jnp.where(last, jnp.concatenate([side, side], 1), moved_base)
        row8 = jnp.broadcast_to(row, (8, nk))
        field[0, m, to, nj : nj + 8, :] = row8
        side8 = pltpu.roll(corner, 127 - at, 1)
        field[1, m, to, nj : nj + 8, :] = jnp.where(
            last8, jnp.concatenate([side8, side8], 1), pltpu.roll(row8, nk - 1, 1)
        )

    def split(f):
        hi = f.astype(BF16).astype(F32)
        return jnp.concatenate([hi, f - hi], 0).astype(BF16)

    sub8 = iota((8, nk), 0)

    def divide(to):
        for jt in range(nj // 8):
            edge = jnp.zeros((8, nk), F32)
            for cm in range(6):
                c, m = divmod(cm, 3)
                f = field[c, m, to, 8 * jt : 8 * jt + 8, :]
                parts[jt, pl.ds(pl.multiple_of(to * 128, 128) + 16 * cm, 16), :] = split(f)
                row = field[c, m, to, 8 * jt + 8 : 8 * jt + 9, :]
                edge = jnp.where(sub8 == cm, jnp.broadcast_to(row, (8, nk)), edge)
            parts[jt, pl.ds(pl.multiple_of(to * 128, 128) + 96, 16), :] = split(edge)
            parts[jt, pl.ds(pl.multiple_of(to * 128, 128) + 112, 16), :] = jnp.zeros((16, nk), BF16)

    def own_plane(i, carry):
        for m in range(3):
            place(
                m, i, u[m, i], ry[m, pl.ds(i, 1), :], rz[0, 0], rz[0, 1, 0:8, :], m * ni + i
            )
        divide(i)
        return carry

    lax.fori_loop(0, ni, own_plane, 0)
    for m in range(3):
        place(m, ni, rx[m], rxy[m, 0:1, :], rz[1, 0], rz[1, 1, 0:8, :], m * ni)
    divide(ni)

    inv_yz = 1.0 / (
        line_sum(me["gy"] * nj + iota((nj, nk), 0), n["gy"] * nj)
        * line_sum(me["gz"] * nk + iota((nj, nk), 1), n["gz"] * nk)
    )
    wy[0, 0:nj, :] = inv_yz

    def plane(i, carry):
        c_sum, v_sum = carry
        inv_x = 1.0 / line_sum(jnp.full((8, nk), me["gx"] * ni + i, jnp.int32), n["gx"] * ni)
        for jt in range(nj // 8):
            data = parts[jt, pl.ds(pl.multiple_of(i * 128, 128), 256), :]
            product = jnp.dot(weights[...], data, preferred_element_type=F32)
            energy = None
            for r in range(24):
                m, a, b, c = r >> 3, (r >> 2) & 1, (r >> 1) & 1, r & 1
                v = product[8 * r : 8 * r + 8] + product[192 + 8 * r : 200 + 8 * r]
                term = v * field[c, m, i + a, 8 * jt + b : 8 * jt + b + 8, :]
                energy = term if energy is None else energy + term
            d = rho[i, 8 * jt : 8 * jt + 8, :]
            c_sum = c_sum + (VOID + d * d * d * (1.0 - VOID)) * energy
            v_sum = v_sum + d
            wx[i + 2, 8 * jt : 8 * jt + 8, :] = (
                (-3.0 * (1.0 - VOID)) * d * d * energy * (inv_x * wy[0, 8 * jt : 8 * jt + 8, :])
            )
        return c_sum, v_sum

    zero = jnp.zeros((8, nk), F32)
    carry = lax.fori_loop(
        0, 4, lambda t, s: plane(jnp.where(t < 2, t, ni - 4 + t), s), (zero, zero)
    )

    def face_copies(axis, base, down_src, up_src, from_up, from_down):
        copies = []
        for at, src, dst, sign in ((base, down_src, from_up, -1), (base + 1, up_src, from_down, 1)):
            copy = pltpu.make_async_remote_copy(
                src_ref=src, dst_ref=dst, send_sem=fsend.at[at], recv_sem=frecv.at[at],
                device_id={axis: me[axis] + sign}, device_id_type=MESH,
            )
            sends = down[axis] if sign < 0 else up[axis]
            takes = up[axis] if sign < 0 else down[axis]
            copies.append((copy, sends, takes, dst))

            @pl.when(sends)
            def _():
                copy.start()

        return copies

    def arrive(copies):
        for copy, sends, takes, dst in copies:

            @pl.when(takes)
            def _():
                copy.wait_recv()

            @pl.when(jnp.logical_not(takes))
            def _():
                dst[...] = jnp.zeros(dst.shape, F32)

    def finish(copies):
        for copy, sends, _, _ in copies:

            @pl.when(sends)
            def _():
                copy.wait_send()

    slot = {"gx": 0, "gy": n["gx"], "gz": n["gx"] + n["gy"]}
    first_sem = {"gx": 0, "gy": n["gx"], "gz": n["gx"] + n["gy"]}

    def share(axis, value):
        mine = slot[axis] + me[axis]
        sums[mine] = value
        copies = []
        for off in range(1, n[axis]):
            copy = pltpu.make_async_remote_copy(
                src_ref=sums.at[mine], dst_ref=sums.at[mine],
                send_sem=gsend.at[first_sem[axis] + off], recv_sem=grecv.at[first_sem[axis] + off],
                device_id={axis: lax.rem(me[axis] + off, n[axis])}, device_id_type=MESH,
            )
            copy.start()
            copies.append(copy)
        return copies

    def gather(axis, copies):
        for copy in copies:
            copy.wait()
        total = sums[slot[axis]]
        for at in range(1, n[axis]):
            total = total + sums[slot[axis] + at]
        return total

    x_copies = face_copies(
        "gx", 0, wx.at[2:4], wx.at[ni : ni + 2], wx.at[ni + 2 : ni + 4], wx.at[0:2]
    )
    c_sum, v_sum = lax.fori_loop(4, ni, lambda t, s: plane(t - 2, s), carry)
    partial = jnp.concatenate([c_sum[:, :128] + c_sum[:, 128:], v_sum[:, :128] + v_sum[:, 128:]], 0)
    x_sums = share("gx", partial)
    arrive(x_copies)

    def smooth_x(i, carry):
        s = 3.0 * wx[i + 2] + 2.0 * (wx[i + 1] + wx[i + 3]) + (wx[i] + wx[i + 4])
        wy[i, 8 : 8 + nj, :] = s
        for at in range(2):
            yslo[at, pl.ds(i, 1), :] = s[at : at + 1]
            yshi[at, pl.ds(i, 1), :] = s[nj - 2 + at : nj - 1 + at]
        return carry

    lax.fori_loop(0, ni, smooth_x, 0)
    y_copies = face_copies("gy", 2, yslo, yshi, ryhi, rylo)
    y_sums = share("gy", gather("gx", x_sums))
    arrive(y_copies)

    def smooth_y(i, carry):
        lo, hi = carry
        for at in range(2):
            wy[i, 6 + at : 7 + at, :] = rylo[at, pl.ds(i, 1), :]
            wy[i, 8 + nj + at : 9 + nj + at, :] = ryhi[at, pl.ds(i, 1), :]
        t = (
            3.0 * wy[i, 8 : 8 + nj, :]
            + 2.0 * (wy[i, 7 : 7 + nj, :] + wy[i, 9 : 9 + nj, :])
            + (wy[i, 6 : 6 + nj, :] + wy[i, 10 : 10 + nj, :])
        )
        out[i] = t
        mine = (lane >> 1) == i
        lo = jnp.where(mine, pltpu.roll(t[:, 0:128], 2 * i, 1), lo)
        hi = jnp.where(mine, pltpu.roll(t[:, nk - 128 : nk], lax.rem(2 * i + 2, 128), 1), hi)
        return lo, hi

    none = jnp.zeros((nj, 128), F32)
    lo, hi = lax.fori_loop(0, ni, smooth_y, (none, none))
    zslo[...] = lo
    zshi[...] = hi
    z_copies = face_copies("gz", 4, zslo, zshi, rzhi, rzlo)
    z_sums = share("gz", gather("gy", y_sums))
    arrive(z_copies)

    lanes = iota((nj, nk), 1)

    def twice(x):
        return jnp.concatenate([x, x], 1)

    def smooth_z(i, carry):
        t = out[i]
        left, right = rzlo[...], rzhi[...]
        a1 = jnp.where(lanes < 1, twice(pltpu.roll(left, 127 - 2 * i, 1)), pltpu.roll(t, 1, 1))
        a2 = jnp.where(lanes < 2, twice(pltpu.roll(left, lax.rem(128 - 2 * i, 128), 1)), pltpu.roll(t, 2, 1))
        b1 = jnp.where(lanes >= nk - 1, twice(pltpu.roll(right, 127 - 2 * i, 1)), pltpu.roll(t, nk - 1, 1))
        b2 = jnp.where(lanes >= nk - 2, twice(pltpu.roll(right, 126 - 2 * i, 1)), pltpu.roll(t, nk - 2, 1))
        out[i] = 3.0 * t + 2.0 * (a1 + b1) + (a2 + b2)
        return carry

    lax.fori_loop(0, ni, smooth_z, 0)
    total = gather("gz", z_sums)
    cells = float(ni * nj * nk * n["gx"] * n["gy"] * n["gz"])
    comp[0, 0] = jnp.sum(total[0:8]) / cells
    vol[0, 0] = jnp.sum(total[8:16]) / cells
    finish(x_copies)
    finish(y_copies)
    finish(z_copies)
    for copy, ok, _, _ in node_copies:

        @pl.when(ok)
        def _():
            copy.wait_send()


def on_device(sizes, displacement, density, stiffness):
    ni, nj, nk = density.shape
    vmem = pl.BlockSpec(memory_space=pltpu.VMEM)
    smem = pl.BlockSpec(memory_space=pltpu.SMEM)
    members = sum(sizes)
    filtered, comp, vol = pl.pallas_call(
        functools.partial(kernel, sizes),
        out_shape=(
            jax.ShapeDtypeStruct((ni, nj, nk), F32),
            jax.ShapeDtypeStruct((1, 1), F32),
            jax.ShapeDtypeStruct((1, 1), F32),
        ),
        in_specs=[vmem] * 3,
        out_specs=(vmem, smem, smem),
        scratch_shapes=[
            pltpu.VMEM((3, nj, nk), F32),
            pltpu.VMEM((3, ni, nk), F32),
            pltpu.VMEM((3, 8, nk), F32),
            pltpu.VMEM((2, 2, nj, 128), F32),
            pltpu.VMEM((3, ni, nk), F32),
            pltpu.VMEM((nj, 128), F32),
            pltpu.VMEM((2, 3, ni + 1, nj + 8, nk), F32),
            pltpu.VMEM((nj // 8, (ni + 1) * 128, nk), BF16),
            pltpu.VMEM((384, 256), BF16),
            pltpu.VMEM((ni + 4, nj, nk), F32),
            pltpu.VMEM((ni, nj + 16, nk), F32),
            pltpu.VMEM((2, ni, nk), F32),
            pltpu.VMEM((2, ni, nk), F32),
            pltpu.VMEM((2, ni, nk), F32),
            pltpu.VMEM((2, ni, nk), F32),
            pltpu.VMEM((nj, 128), F32),
            pltpu.VMEM((nj, 128), F32),
            pltpu.VMEM((nj, 128), F32),
            pltpu.VMEM((nj, 128), F32),
            pltpu.VMEM((members, 16, 128), F32),
            pltpu.SemaphoreType.DMA((7,)),
            pltpu.SemaphoreType.DMA((7,)),
            pltpu.SemaphoreType.DMA((6,)),
            pltpu.SemaphoreType.DMA((6,)),
            pltpu.SemaphoreType.DMA((members,)),
            pltpu.SemaphoreType.DMA((members,)),
        ],
        compiler_params=pltpu.CompilerParams(
            collective_id=0, has_side_effects=True, vmem_limit_bytes=60 * 1024 * 1024
        ),
    )(displacement, density, stiffness)
    return filtered, comp.reshape(()), vol.reshape(())


def solution(mesh):
    sizes = tuple(mesh.shape[axis] for axis in AXES)
    return jax.shard_map(
        functools.partial(on_device, sizes),
        mesh=mesh,
        in_specs=(P(None, "gx", "gy", "gz"), P("gx", "gy", "gz"), P()),
        out_specs=(P("gx", "gy", "gz"), P(), P()),
        check_vma=False,
    )
```

time: 209 us -> 37.7 us (0.18)
  the two profiles are of different devices: /device:TPU:0 before, /device:TPU:1 now
where the time goes in v1:
time: 37.7 us; the launch traced here: 37.5 us
  Pallas kernels  31.5 us (84%)
  between operations  4.1 us (11%)
  local copies, waits for them, and re-layouts  1.88 us (5%)
    pallas_call x1, Pallas kernels, on_device(): pl.pallas_call(functools.partial(kernel, sizes), out_shape=(jax.ShapeDtyp...  31.5 us
    unnamed x1, local copies, waits for them, and re-layouts  1.88 us

profile of v1, /device:TPU:1, one launch (start us, length us, event | category | flops | bytes accessed | tf_op | source)
XLA Modules:
  0.0 37.5 jit_solution(15864242709225197739)
XLA Ops:
  0.6 31.5 %shard_map.58 = (f32[16,32,256]{2,1,0:T(8,128)}, f32[1,1]{1,0:T(1,128)}, f32[1,1]{1,0:T(1,128)}) custom-call(f32[3,16,32,256]{3,2,1,0:T(8,128)} %u.1, f32[16,32,256]{2,1,0:T(8,128)} %rho.1, f32[24,24]{1,0:T(8,128)} %stiff.1), custom_call_target="tpu_custom_call" | custom-call | tf_op jit(solution)/shard_map/pallas_call | solution.py:365
  32.1 1.9 %copy.9 = f32[16,32,256]{2,1,0:T(8,128)} copy(f32[16,32,256]{2,1,0:T(8,128)} %get-tuple-element.12) | data formatting | bytes 1048576

commit v2 on v1

v2 whole, which is shorter than its diff:
```python
import functools

import jax
import jax.numpy as jnp
from jax import lax
from jax.experimental import pallas as pl
from jax.experimental.pallas import tpu as pltpu
from jax.sharding import PartitionSpec as P

VOID = 0.001
H = (1.0, 2.0, 3.0, 2.0, 1.0)
MESH = pl.DeviceIdType.MESH
AXES = ("gx", "gy", "gz")
F32 = jnp.float32
BF16 = jnp.bfloat16
NODE_STEPS = [(a, b, c) for a in (0, 1) for b in (0, 1) for c in (0, 1) if a + b + c]
SIDE_STEPS = [(b, c) for b in (-1, 0, 1) for c in (-1, 0, 1) if b or c]


def iota(shape, dim):
    return lax.broadcasted_iota(jnp.int32, shape, dim)


def line_sum(position, extent):
    total = None
    for d in range(5):
        at = position + (d - 2)
        term = jnp.where((at >= 0) & (at < extent), H[d], 0.0).astype(F32)
        total = term if total is None else total + term
    return total


def band_weights(stiff):
    rows, cols = 192, 256
    pick = jnp.where((iota((rows, 24), 0) >> 3) == iota((rows, 24), 1), 1.0, 0.0).astype(F32)

    def column(shape):
        col = iota(shape, 1)
        a, g, s = col >> 7, (col >> 4) & 7, col & 7
        cm = jnp.where(g == 6, s, g)
        c = jnp.where(cm >= 3, 1, 0)
        m = cm - 3 * c
        valid = (g < 6) | ((g == 6) & (s < 6))
        return 8 * m + 4 * a + c, valid, jnp.where(g == 6, 8, s), (col >> 3) & 1

    total = None
    for b in (0, 1):
        q, valid, _, _ = column((24, cols))
        place = jnp.where((iota((24, cols), 0) == q + 2 * b) & valid, 1.0, 0.0).astype(F32)
        wide = jnp.dot(stiff, place, precision=lax.Precision.HIGHEST, preferred_element_type=F32)
        tall = jnp.dot(pick, wide, precision=lax.Precision.HIGHEST, preferred_element_type=F32)
        _, _, jj, _ = column((rows, cols))
        term = jnp.where(jj - (iota((rows, cols), 0) & 7) == b, tall, 0.0)
        total = term if total is None else total + term
    high = total.astype(BF16).astype(F32)
    _, _, _, lo_col = column((rows, cols))
    low = jnp.where(lo_col == 0, total - high, 0.0)
    return high.astype(BF16), low.astype(BF16)


def kernel(
    sizes, u_hbm, rho_hbm, stiff_hbm, out, packs, totals,
    u, rho, stiff, rx, ry, rxy, rz, ys, zs, field, parts, weights, wx, wy,
    yslo, yshi, rylo, ryhi, zslo, zshi, rzz, sums, insem, nsend, nrecv, fsend, frecv, gsend, grecv,
):
    ni, nj, nk = rho.shape
    n = dict(zip(AXES, sizes))
    me = {axis: lax.axis_index(axis) for axis in AXES}
    ny, nz = n["gy"], n["gz"]
    down = {axis: me[axis] > 0 for axis in AXES}
    up = {axis: me[axis] < n[axis] - 1 for axis in AXES}

    loads = []
    for at, (src, dst) in enumerate(((stiff_hbm, stiff), (u_hbm, u), (rho_hbm, rho))):
        copy = pltpu.make_async_copy(src, dst, insem.at[at])
        copy.start()
        loads.append(copy)

    def hop(step):
        ids, ok = {}, None
        for axis, s in zip(AXES, step):
            if s:
                ids[axis] = me[axis] + s
                flag = up[axis] if s > 0 else down[axis]
                ok = flag if ok is None else jnp.logical_and(ok, flag)
        return ids, ok

    def minus(step):
        return tuple(-s for s in step)

    line = [{"gx": lax.rem(me["gx"] + off, n["gx"])} for off in range(1, n["gx"])]
    sheet = [
        {"gy": lax.rem(me["gy"] + off // nz, ny), "gz": lax.rem(me["gz"] + off % nz, nz)}
        for off in range(1, ny * nz)
    ]
    barrier = pltpu.get_barrier_semaphore()
    for ids in line + sheet:
        pl.semaphore_signal(barrier, inc=1, device_id=ids, device_id_type=MESH)
    peers = len(line) + len(sheet)
    for step in NODE_STEPS:
        if step[0] and sum(step) > 1:
            for way in (step, minus(step)):
                ids, ok = hop(way)
                peers = peers + jnp.where(ok, 1, 0)

                @pl.when(ok)
                def _():
                    pl.semaphore_signal(barrier, inc=1, device_id=ids, device_id_type=MESH)

    loads[0].wait()
    high, low = band_weights(stiff[...])
    weights[0:192, :] = high
    weights[192:384, :] = low

    loads[1].wait()
    lane = iota((nj, 128), 1)
    for m in range(3):
        for i in range(ni):
            ys[m, i : i + 1, :] = u[m, i, 0:1, :]

    def pack(i, acc):
        for m in range(3):
            at = m * ni + i
            acc = jnp.where(lane == at, pltpu.roll(u[m, i, :, 0:128], at, 1), acc)
        return acc

    zs[...] = lax.fori_loop(0, ni, pack, jnp.zeros((nj, 128), F32))
    pl.semaphore_wait(barrier, peers)

    def swap(copies, src, dst, send_sem, recv_sem, step):
        ids, sends = hop(step)
        copy = pltpu.make_async_remote_copy(
            src_ref=src, dst_ref=dst, send_sem=send_sem, recv_sem=recv_sem,
            device_id=ids, device_id_type=MESH,
        )
        copies.append((copy, sends, hop(minus(step))[1], dst))

        @pl.when(sends)
        def _():
            copy.start()

    def arrive(copies):
        for copy, _, takes, dst in copies:

            @pl.when(takes)
            def _():
                copy.wait_recv()

            @pl.when(jnp.logical_not(takes))
            def _():
                dst[...] = jnp.zeros(dst.shape, F32)

    def finish(copies):
        for copy, sends, _, _ in copies:

            @pl.when(sends)
            def _():
                copy.wait_send()

    near, far = [], []
    for at, step in enumerate(NODE_STEPS):
        a, b, c = step
        if c:
            src, dst = zs, rz.at[a, b]
        elif b:
            src, dst = (ys.at[:, 0:8, :], rxy) if a else (ys, ry)
        else:
            src, dst = u.at[:, 0], rx
        swap(far if a else near, src, dst, nsend.at[at], nrecv.at[at], minus(step))

    last = iota((nj, nk), 1) == nk - 1
    last8 = iota((8, nk), 1) == nk - 1
    sub8 = iota((8, nk), 0)

    def split(f):
        hi = f.astype(BF16).astype(F32)
        return jnp.concatenate([hi, f - hi], 0).astype(BF16)

    def put(jt, to, at, f):
        parts[jt, pl.ds(pl.multiple_of(to * 128, 128) + at, 16), :] = split(f)

    def first_half(m, to, base):
        field[0, m, to, 0:nj, :] = base
        for jt in range(nj // 8):
            put(jt, to, 16 * m, base[8 * jt : 8 * jt + 8])

    def second_half(m, to, base, row, col, corner, at):
        side = pltpu.roll(col, 127 - at, 1)
        moved = jnp.where(last, jnp.concatenate([side, side], 1), pltpu.roll(base, nk - 1, 1))
        field[1, m, to, 0:nj, :] = moved
        for jt in range(nj // 8):
            put(jt, to, 48 + 16 * m, moved[8 * jt : 8 * jt + 8])
        row8 = jnp.broadcast_to(row, (8, nk))
        field[0, m, to, nj : nj + 8, :] = row8
        side8 = pltpu.roll(corner, 127 - at, 1)
        field[1, m, to, nj : nj + 8, :] = jnp.where(
            last8, jnp.concatenate([side8, side8], 1), pltpu.roll(row8, nk - 1, 1)
        )

    def edges(to):
        for jt in range(nj // 8):
            edge = jnp.zeros((8, nk), F32)
            for cm in range(6):
                c, m = divmod(cm, 3)
                row = field[c, m, to, 8 * jt + 8 : 8 * jt + 9, :]
                edge = jnp.where(sub8 == cm, jnp.broadcast_to(row, (8, nk)), edge)
            put(jt, to, 96, edge)

    def own_first(i, carry):
        for m in range(3):
            first_half(m, i, u[m, i])
        for jt in range(nj // 8):
            parts[jt, pl.ds(pl.multiple_of(i * 128, 128) + 112, 16), :] = jnp.zeros((16, nk), BF16)
        return carry

    def own_second(i, carry):
        for m in range(3):
            second_half(
                m, i, u[m, i], ry[m, pl.ds(i, 1), :], rz[0, 0], rz[0, 1, 0:8, :], m * ni + i
            )
        edges(i)
        return carry

    lax.fori_loop(0, ni, own_first, 0)
    for jt in range(nj // 8):
        parts[jt, ni * 128 + 112 : ni * 128 + 128, :] = jnp.zeros((16, nk), BF16)
    loads[2].wait()
    wy[0, 0:nj, :] = 1.0 / (
        line_sum(me["gy"] * nj + iota((nj, nk), 0), ny * nj)
        * line_sum(me["gz"] * nk + iota((nj, nk), 1), nz * nk)
    )
    arrive(near)
    lax.fori_loop(0, ni, own_second, 0)
    arrive(far)
    for m in range(3):
        first_half(m, ni, rx[m])
        second_half(m, ni, rx[m], rxy[m, 0:1, :], rz[1, 0], rz[1, 1, 0:8, :], m * ni)
    edges(ni)

    def plane(i, carry):
        c_sum, v_sum = carry
        inv_x = 1.0 / line_sum(jnp.full((8, nk), me["gx"] * ni + i, jnp.int32), n["gx"] * ni)
        for jt in range(nj // 8):
            data = parts[jt, pl.ds(pl.multiple_of(i * 128, 128), 256), :]
            product = jnp.dot(weights[...], data, preferred_element_type=F32)
            energy = None
            for r in range(24):
                m, a, b, c = r >> 3, (r >> 2) & 1, (r >> 1) & 1, r & 1
                v = product[8 * r : 8 * r + 8] + product[192 + 8 * r : 200 + 8 * r]
                term = v * field[c, m, i + a, 8 * jt + b : 8 * jt + b + 8, :]
                energy = term if energy is None else energy + term
            d = rho[i, 8 * jt : 8 * jt + 8, :]
            c_sum = c_sum + (VOID + d * d * d * (1.0 - VOID)) * energy
            v_sum = v_sum + d
            wx[i + 2, 8 * jt : 8 * jt + 8, :] = (
                (-3.0 * (1.0 - VOID)) * d * d * energy * (inv_x * wy[0, 8 * jt : 8 * jt + 8, :])
            )
        return c_sum, v_sum

    zero = jnp.zeros((8, nk), F32)
    carry = lax.fori_loop(
        0, 4, lambda t, s: plane(jnp.where(t < 2, t, ni - 4 + t), s), (zero, zero)
    )
    x_copies = []
    swap(x_copies, wx.at[2:4], wx.at[ni + 2 : ni + 4], fsend.at[8], frecv.at[8], (-1, 0, 0))
    swap(x_copies, wx.at[ni : ni + 2], wx.at[0:2], fsend.at[9], frecv.at[9], (1, 0, 0))
    c_sum, v_sum = lax.fori_loop(4, ni, lambda t, s: plane(t - 2, s), carry)

    def share(base, mine, value, group):
        sums[base + mine] = value
        copies = []
        for off, ids in enumerate(group):
            copy = pltpu.make_async_remote_copy(
                src_ref=sums.at[base + mine], dst_ref=sums.at[base + mine],
                send_sem=gsend.at[base + off], recv_sem=grecv.at[base + off],
                device_id=ids, device_id_type=MESH,
            )
            copy.start()
            copies.append(copy)
        return copies

    def gather(base, copies):
        for copy in copies:
            copy.wait()
        total = sums[base]
        for at in range(1, len(copies) + 1):
            total = total + sums[base + at]
        return total

    partial = jnp.concatenate([c_sum[:, :128] + c_sum[:, 128:], v_sum[:, :128] + v_sum[:, 128:]], 0)
    x_sums = share(0, me["gx"], partial, line)
    arrive(x_copies)

    def smooth_x(i, carry):
        lo, hi = carry
        s = 3.0 * wx[i + 2] + 2.0 * (wx[i + 1] + wx[i + 3]) + (wx[i] + wx[i + 4])
        wy[i, 8 : 8 + nj, :] = s
        for at in range(2):
            yslo[at, pl.ds(i, 1), :] = s[at : at + 1]
            yshi[at, pl.ds(i, 1), :] = s[nj - 2 + at : nj - 1 + at]
        mine = (lane >> 1) == i
        lo = jnp.where(mine, pltpu.roll(s[:, 0:128], 2 * i, 1), lo)
        hi = jnp.where(mine, pltpu.roll(s[:, nk - 128 : nk], lax.rem(2 * i + 2, 128), 1), hi)
        return lo, hi

    none = jnp.zeros((nj, 128), F32)
    lo, hi = lax.fori_loop(0, ni, smooth_x, (none, none))
    zslo[...] = lo
    zshi[...] = hi
    side_copies = []
    for at, (b, c) in enumerate(SIDE_STEPS):
        if c:
            rows = (slice(nj - 8, nj), slice(0, nj), slice(0, 8))[1 - b]
            to = (slice(0, 8), slice(8, 8 + nj), slice(8 + nj, 16 + nj))[1 - b]
            src = (zslo if c < 0 else zshi).at[rows]
            dst = rzz.at[1 if c < 0 else 0, to]
        else:
            src, dst = (yslo, ryhi) if b < 0 else (yshi, rylo)
        swap(side_copies, src, dst, fsend.at[at], frecv.at[at], (0, b, c))
    all_sums = share(n["gx"], me["gy"] * nz + me["gz"], gather(0, x_sums), sheet)
    arrive(side_copies)

    def smooth_rows(ref, at):
        return (
            3.0 * ref[at, 8 : 8 + nj, :]
            + 2.0 * (ref[at, 7 : 7 + nj, :] + ref[at, 9 : 9 + nj, :])
            + (ref[at, 6 : 6 + nj, :] + ref[at, 10 : 10 + nj, :])
        )

    for side in range(2):
        packs[side] = smooth_rows(rzz, side)

    def smooth_y(i, carry):
        for at in range(2):
            wy[i, 6 + at : 7 + at, :] = rylo[at, pl.ds(i, 1), :]
            wy[i, 8 + nj + at : 9 + nj + at, :] = ryhi[at, pl.ds(i, 1), :]
        out[i] = smooth_rows(wy, i)
        return carry

    lax.fori_loop(0, ni, smooth_y, 0)
    totals[...] = gather(n["gx"], all_sums)
    for copies in (near, far, x_copies, side_copies):
        finish(copies)


def last_pass(cells, field, packs, totals, out, comp, vol):
    ni, nj, nk = field.shape
    comp[0, 0] = jnp.sum(totals[0:8]) / cells
    vol[0, 0] = jnp.sum(totals[8:16]) / cells
    lanes = iota((nj, nk), 1)

    def twice(x):
        return jnp.concatenate([x, x], 1)

    def smooth_z(i, carry):
        t = field[i]
        left, right = packs[0], packs[1]
        a1 = jnp.where(lanes < 1, twice(pltpu.roll(left, 127 - 2 * i, 1)), pltpu.roll(t, 1, 1))
        a2 = jnp.where(lanes < 2, twice(pltpu.roll(left, lax.rem(128 - 2 * i, 128), 1)), pltpu.roll(t, 2, 1))
        b1 = jnp.where(lanes >= nk - 1, twice(pltpu.roll(right, 127 - 2 * i, 1)), pltpu.roll(t, nk - 1, 1))
        b2 = jnp.where(lanes >= nk - 2, twice(pltpu.roll(right, 126 - 2 * i, 1)), pltpu.roll(t, nk - 2, 1))
        out[i] = 3.0 * t + 2.0 * (a1 + b1) + (a2 + b2)
        return carry

    lax.fori_loop(0, ni, smooth_z, 0)


def on_device(sizes, displacement, density, stiffness):
    ni, nj, nk = density.shape
    vmem = pl.BlockSpec(memory_space=pltpu.VMEM)
    smem = pl.BlockSpec(memory_space=pltpu.SMEM)
    hbm = pl.BlockSpec(memory_space=pltpu.HBM)
    members = sizes[0] + sizes[1] * sizes[2]
    scratch = [
        displacement.shape, density.shape, stiffness.shape,
        (3, nj, nk), (3, ni, nk), (3, 8, nk), (2, 2, nj, 128), (3, ni, nk), (nj, 128),
        (2, 3, ni + 1, nj + 8, nk),
    ]
    later = [
        (ni + 4, nj, nk), (ni, nj + 16, nk),
        (2, ni, nk), (2, ni, nk), (2, ni, nk), (2, ni, nk),
        (nj, 128), (nj, 128), (2, nj + 16, 128), (members, 16, 128),
    ]
    field, packs, totals = pl.pallas_call(
        functools.partial(kernel, sizes),
        out_shape=(
            jax.ShapeDtypeStruct((ni, nj, nk), F32),
            jax.ShapeDtypeStruct((2, nj, 128), F32),
            jax.ShapeDtypeStruct((16, 128), F32),
        ),
        in_specs=[hbm] * 3,
        out_specs=(vmem, vmem, vmem),
        scratch_shapes=[pltpu.VMEM(shape, F32) for shape in scratch]
        + [pltpu.VMEM((nj // 8, (ni + 1) * 128, nk), BF16), pltpu.VMEM((384, 256), BF16)]
        + [pltpu.VMEM(shape, F32) for shape in later]
        + [pltpu.SemaphoreType.DMA((count,)) for count in (3, 7, 7, 10, 10, members, members)],
        compiler_params=pltpu.CompilerParams(
            collective_id=0, has_side_effects=True, vmem_limit_bytes=24 * 1024 * 1024
        ),
    )(displacement, density, stiffness)
    cells = float(ni * nj * nk * sizes[0] * sizes[1] * sizes[2])
    filtered, comp, vol = pl.pallas_call(
        functools.partial(last_pass, cells),
        out_shape=(
            jax.ShapeDtypeStruct((ni, nj, nk), F32),
            jax.ShapeDtypeStruct((1, 1), F32),
            jax.ShapeDtypeStruct((1, 1), F32),
        ),
        in_specs=[vmem] * 3,
        out_specs=(vmem, smem, smem),
        compiler_params=pltpu.CompilerParams(vmem_limit_bytes=24 * 1024 * 1024),
    )(field, packs, totals)
    return filtered, comp.reshape(()), vol.reshape(())


def solution(mesh):
    sizes = tuple(mesh.shape[axis] for axis in AXES)
    return jax.shard_map(
        functools.partial(on_device, sizes),
        mesh=mesh,
        in_specs=(P(None, "gx", "gy", "gz"), P("gx", "gy", "gz"), P()),
        out_specs=(P("gx", "gy", "gz"), P(), P()),
        check_vma=False,
    )
```

time: 37.7 us -> 31.5 us (0.84)
  the two profiles are of different devices: /device:TPU:1 before, /device:TPU:0 now
where the time goes in v2:
time: 31.5 us; the launch traced here: 31.2 us
  Pallas kernels  27.4 us (87%)
  local copies, waits for them, and re-layouts  3.15 us (10%)
  between operations  0.65 us (2%)
    pallas_call x1, Pallas kernels, on_device(): pl.pallas_call(functools.partial(kernel, sizes), out_shape=(jax.ShapeDtyp...  24.6 us
    unnamed x6, local copies, waits for them, and re-layouts  3.15 us
    pallas_call x1, Pallas kernels, on_device(): pl.pallas_call(functools.partial(last_pass, cells), out_shape=(jax.ShapeD...  2.85 us

profile of v2, /device:TPU:0, one launch (start us, length us, event | category | flops | bytes accessed | tf_op | source)
XLA Modules:
  0.0 31.2 jit_solution(4145113877987440046)
XLA Ops:
  0.6 0.0 copy-start
  0.6 1.4 %copy-done = f32[3,16,32,256]{3,2,1,0:T(8,128)S(1)} copy-done((f32[3,16,32,256]{3,2,1,0:T(8,128)S(1)}, f32[3,16,32,256]{3,2,1,0:T(8,128)}, u32[]{:S(2)}) %copy-start) | copy-done | bytes 1572888
  2.0 0.0 copy-start.1
  2.0 1.0 %copy-done.1 = f32[16,32,256]{2,1,0:T(8,128)S(1)} copy-done((f32[16,32,256]{2,1,0:T(8,128)S(1)}, f32[16,32,256]{2,1,0:T(8,128)}, u32[]{:S(2)}) %copy-start.1) | copy-done | bytes 524312
  3.1 0.0 copy-start.2
  3.1 0.7 %copy-done.2 = f32[24,24]{1,0:T(8,128)S(1)} copy-done((f32[24,24]{1,0:T(8,128)S(1)}, f32[24,24]{1,0:T(8,128)}, u32[]{:S(2)}) %copy-start.2) | copy-done | bytes 2328
  3.8 24.6 %shard_map.58 = (f32[16,32,256]{2,1,0:T(8,128)S(1)}, f32[2,32,128]{2,1,0:T(8,128)S(1)}, f32[16,128]{1,0:T(8,128)S(1)}) custom-call(f32[3,16,32,256]{3,2,1,0:T(8,128)S(1)} %copy-done, f32[16,32,256]{2,1,0:T(8,128)S(1)} %copy-done.1, f32[24,24]{1,0:T(8,128)S(1)} %copy-done.2), custom_call_target="tpu_custom_call" | custom-call | tf_op jit(solution)/shard_map/pallas_call | solution.py:384
  28.4 2.9 %shard_map.59 = (f32[16,32,256]{2,1,0:T(8,128)}, f32[1,1]{1,0:T(1,128)}, f32[1,1]{1,0:T(1,128)}) custom-call(f32[16,32,256]{2,1,0:T(8,128)S(1)} %get-tuple-element.9.field, f32[2,32,128]{2,1,0:T(8,128)S(1)} %get-tuple-element.10.packs, f32[16,128]{1,0:T(8,128)S(1)} %get-tuple-element.11.totals), custom_call_target="tpu_custom_call" | custom-call | tf_op jit(solution)/shard_map/pallas_call | solution.py:402
Async XLA Ops:
  0.6 1.4 %copy-start = (f32[3,16,32,256]{3,2,1,0:T(8,128)S(1)}, f32[3,16,32,256]{3,2,1,0:T(8,128)}, u32[]{:S(2)}) copy-start(f32[3,16,32,256]{3,2,1,0:T(8,128)} %u_hbm.1) | copy-start | bytes 4718596
  2.0 1.0 %copy-start.1 = (f32[16,32,256]{2,1,0:T(8,128)S(1)}, f32[16,32,256]{2,1,0:T(8,128)}, u32[]{:S(2)}) copy-start(f32[16,32,256]{2,1,0:T(8,128)} %rho_hbm.1) | copy-start | bytes 1572868
  3.1 0.7 %copy-start.2 = (f32[24,24]{1,0:T(8,128)S(1)}, f32[24,24]{1,0:T(8,128)}, u32[]{:S(2)}) copy-start(f32[24,24]{1,0:T(8,128)} %stiff_hbm.1) | copy-start | bytes 6916

commit v3 on v2

--- a/solution.py
+++ b/solution.py
@@ -397,7 +397,7 @@
         compiler_params=pltpu.CompilerParams(
             collective_id=0, has_side_effects=True, vmem_limit_bytes=24 * 1024 * 1024
         ),
-    )(displacement, density, stiffness)
+    )(*(pltpu.with_memory_space_constraint(x, pltpu.HBM) for x in (displacement, density, stiffness)))
     cells = float(ni * nj * nk * sizes[0] * sizes[1] * sizes[2])
     filtered, comp, vol = pl.pallas_call(
         functools.partial(last_pass, cells),

time: 31.5 us -> 28.8 us (0.914)
  local copies, waits for them, and re-layouts: 3.15 us -> 0 us
  Pallas kernels: 27.4 us -> 27.9 us
    unnamed x6 -> x0, local copies, waits for them, and re-layouts: 3.15 us -> none
    pallas_call x1, Pallas kernels: 24.6 us -> 25.1 us  [on_device(): pl.pallas_call(functools.partial(kernel, sizes), out_shape=(jax.ShapeDtyp...]
where the time goes in v3:
time: 28.8 us; the launch traced here: 28.6 us
  Pallas kernels  27.9 us (97%)
  between operations  0.64 us (2%)
    pallas_call x1, Pallas kernels, on_device(): pl.pallas_call(functools.partial(kernel, sizes), out_shape=(jax.ShapeDtyp...  25.1 us
    pallas_call x1, Pallas kernels, on_device(): pl.pallas_call(functools.partial(last_pass, cells), out_shape=(jax.ShapeD...  2.85 us

profile of v3, /device:TPU:0, one launch (start us, length us, event | category | flops | bytes accessed | tf_op | source)
XLA Modules:
  0.0 28.6 jit_solution(5935639862082772763)
XLA Ops:
  0.6 25.1 %shard_map.58 = (f32[16,32,256]{2,1,0:T(8,128)S(1)}, f32[2,32,128]{2,1,0:T(8,128)S(1)}, f32[16,128]{1,0:T(8,128)S(1)}) custom-call(f32[3,16,32,256]{3,2,1,0:T(8,128)} %u_hbm.1, f32[16,32,256]{2,1,0:T(8,128)} %rho_hbm.1, f32[24,24]{1,0:T(8,128)} %stiff_hbm.1), custom_call_target="tpu_custom_call" | custom-call | tf_op jit(solution)/shard_map/pallas_call | solution.py:384
  25.7 2.9 %shard_map.59 = (f32[16,32,256]{2,1,0:T(8,128)}, f32[1,1]{1,0:T(1,128)}, f32[1,1]{1,0:T(1,128)}) custom-call(f32[16,32,256]{2,1,0:T(8,128)S(1)} %get-tuple-element.9.field, f32[2,32,128]{2,1,0:T(8,128)S(1)} %get-tuple-element.10.packs, f32[16,128]{1,0:T(8,128)S(1)} %get-tuple-element.11.totals), custom_call_target="tpu_custom_call" | custom-call | tf_op jit(solution)/shard_map/pallas_call | solution.py:402

commit v4 on v3

--- a/solution.py
+++ b/solution.py
@@ -60,7 +60,7 @@
 
 def kernel(
     sizes, u_hbm, rho_hbm, stiff_hbm, out, packs, totals,
-    u, rho, stiff, rx, ry, rxy, rz, ys, zs, field, parts, weights, wx, wy,
+    u, rho, stiff, rx, ry, rxy, rz, ys, yd, zs, field, parts, weights, wx, wy,
     yslo, yshi, rylo, ryhi, zslo, zshi, rzz, sums, insem, nsend, nrecv, fsend, frecv, gsend, grecv,
 ):
     ni, nj, nk = rho.shape
@@ -107,24 +107,6 @@
                 def _():
                     pl.semaphore_signal(barrier, inc=1, device_id=ids, device_id_type=MESH)
 
-    loads[0].wait()
-    high, low = band_weights(stiff[...])
-    weights[0:192, :] = high
-    weights[192:384, :] = low
-
-    loads[1].wait()
-    lane = iota((nj, 128), 1)
-    for m in range(3):
-        for i in range(ni):
-            ys[m, i : i + 1, :] = u[m, i, 0:1, :]
-
-    def pack(i, acc):
-        for m in range(3):
-            at = m * ni + i
-            acc = jnp.where(lane == at, pltpu.roll(u[m, i, :, 0:128], at, 1), acc)
-        return acc
-
-    zs[...] = lax.fori_loop(0, ni, pack, jnp.zeros((nj, 128), F32))
     pl.semaphore_wait(barrier, peers)
 
     def swap(copies, src, dst, send_sem, recv_sem, step):
@@ -157,16 +139,45 @@
             def _():
                 copy.wait_send()
 
-    near, far = [], []
-    for at, step in enumerate(NODE_STEPS):
+    beside, below, far = [], [], []
+
+    def node_swap(step):
         a, b, c = step
+        at = NODE_STEPS.index(step)
         if c:
-            src, dst = zs, rz.at[a, b]
+            src, dst = (zs.at[0:8], rz.at[a, b, 0:8]) if b else (zs, rz.at[a, b])
         elif b:
-            src, dst = (ys.at[:, 0:8, :], rxy) if a else (ys, ry)
+            src, dst = (yd, rxy) if a else (ys, ry)
         else:
-            src, dst = u.at[:, 0], rx
-        swap(far if a else near, src, dst, nsend.at[at], nrecv.at[at], minus(step))
+            src, dst = u_hbm.at[:, 0], rx
+        copies = far if a else (below if b else beside)
+        swap(copies, src, dst, nsend.at[at], nrecv.at[at], minus(step))
+
+    node_swap((1, 0, 0))
+    loads[1].wait()
+    lane = iota((nj, 128), 1)
+    yd[...] = jnp.zeros(yd.shape, F32)
+    for m in range(3):
+        for i in range(ni):
+            ys[m, i : i + 1, :] = u[m, i, 0:1, :]
+        yd[m : m + 1, :] = u[m, 0, 0:1, :]
+    node_swap((0, 1, 0))
+    node_swap((1, 1, 0))
+
+    def pack(i, acc):
+        for m in range(3):
+            at = m * ni + i
+            acc = jnp.where(lane == at, pltpu.roll(u[m, i, :, 0:128], at, 1), acc)
+        return acc
+
+    zs[...] = lax.fori_loop(0, ni, pack, jnp.zeros((nj, 128), F32))
+    for step in NODE_STEPS:
+        if step[2]:
+            node_swap(step)
+    loads[0].wait()
+    high, low = band_weights(stiff[...])
+    weights[0:192, :] = high
+    weights[192:384, :] = low
 
     last = iota((nj, nk), 1) == nk - 1
     last8 = iota((8, nk), 1) == nk - 1
@@ -184,12 +195,14 @@
         for jt in range(nj // 8):
             put(jt, to, 16 * m, base[8 * jt : 8 * jt + 8])
 
-    def second_half(m, to, base, row, col, corner, at):
+    def second_half(m, to, base, col, at):
         side = pltpu.roll(col, 127 - at, 1)
         moved = jnp.where(last, jnp.concatenate([side, side], 1), pltpu.roll(base, nk - 1, 1))
         field[1, m, to, 0:nj, :] = moved
         for jt in range(nj // 8):
             put(jt, to, 48 + 16 * m, moved[8 * jt : 8 * jt + 8])
+
+    def next_row(m, to, row, corner, at):
         row8 = jnp.broadcast_to(row, (8, nk))
         field[0, m, to, nj : nj + 8, :] = row8
         side8 = pltpu.roll(corner, 127 - at, 1)
@@ -215,9 +228,12 @@
 
     def own_second(i, carry):
         for m in range(3):
-            second_half(
-                m, i, u[m, i], ry[m, pl.ds(i, 1), :], rz[0, 0], rz[0, 1, 0:8, :], m * ni + i
-            )
+            second_half(m, i, u[m, i], rz[0, 0], m * ni + i)
+        return carry
+
+    def own_edges(i, carry):
+        for m in range(3):
+            next_row(m, i, ry[m, pl.ds(i, 1), :], rz[0, 1, 0:8, :], m * ni + i)
         edges(i)
         return carry
 
@@ -229,12 +245,15 @@
         line_sum(me["gy"] * nj + iota((nj, nk), 0), ny * nj)
         * line_sum(me["gz"] * nk + iota((nj, nk), 1), nz * nk)
     )
-    arrive(near)
+    arrive(beside)
     lax.fori_loop(0, ni, own_second, 0)
+    arrive(below)
+    lax.fori_loop(0, ni, own_edges, 0)
     arrive(far)
     for m in range(3):
         first_half(m, ni, rx[m])
-        second_half(m, ni, rx[m], rxy[m, 0:1, :], rz[1, 0], rz[1, 1, 0:8, :], m * ni)
+        second_half(m, ni, rx[m], rz[1, 0], m * ni)
+        next_row(m, ni, rxy[m : m + 1, :], rz[1, 1, 0:8, :], m * ni)
     edges(ni)
 
     def plane(i, carry):
@@ -339,7 +358,7 @@
 
     lax.fori_loop(0, ni, smooth_y, 0)
     totals[...] = gather(n["gx"], all_sums)
-    for copies in (near, far, x_copies, side_copies):
+    for copies in (beside, below, far, x_copies, side_copies):
         finish(copies)
 
 
@@ -373,7 +392,7 @@
     members = sizes[0] + sizes[1] * sizes[2]
     scratch = [
         displacement.shape, density.shape, stiffness.shape,
-        (3, nj, nk), (3, ni, nk), (3, 8, nk), (2, 2, nj, 128), (3, ni, nk), (nj, 128),
+        (3, nj, nk), (3, ni, nk), (8, nk), (2, 2, nj, 128), (3, ni, nk), (8, nk), (nj, 128),
         (2, 3, ni + 1, nj + 8, nk),
     ]
     later = [

time: 28.8 us -> 28.5 us (0.990)
  no operation moved by 1% of the time
where the time goes in v4:
time: 28.5 us; the launch traced here: 28.4 us
  Pallas kernels  27.8 us (98%)
  between operations  0.64 us (2%)
    pallas_call x1, Pallas kernels, on_device(): pl.pallas_call(functools.partial(kernel, sizes), out_shape=(jax.ShapeDtyp...  24.9 us
    pallas_call x1, Pallas kernels, on_device(): pl.pallas_call(functools.partial(last_pass, cells), out_shape=(jax.ShapeD...  2.85 us

profile of v4, /device:TPU:0, one launch (start us, length us, event | category | flops | bytes accessed | tf_op | source)
XLA Modules:
  0.0 28.4 jit_solution(16494252184902246390)
XLA Ops:
  0.6 24.9 %shard_map.58 = (f32[16,32,256]{2,1,0:T(8,128)S(1)}, f32[2,32,128]{2,1,0:T(8,128)S(1)}, f32[16,128]{1,0:T(8,128)S(1)}) custom-call(f32[3,16,32,256]{3,2,1,0:T(8,128)} %u_hbm.1, f32[16,32,256]{2,1,0:T(8,128)} %rho_hbm.1, f32[24,24]{1,0:T(8,128)} %stiff_hbm.1), custom_call_target="tpu_custom_call" | custom-call | tf_op jit(solution)/shard_map/pallas_call | solution.py:403
  25.5 2.9 %shard_map.59 = (f32[16,32,256]{2,1,0:T(8,128)}, f32[1,1]{1,0:T(1,128)}, f32[1,1]{1,0:T(1,128)}) custom-call(f32[16,32,256]{2,1,0:T(8,128)S(1)} %get-tuple-element.9.field, f32[2,32,128]{2,1,0:T(8,128)S(1)} %get-tuple-element.10.packs, f32[16,128]{1,0:T(8,128)S(1)} %get-tuple-element.11.totals), custom_call_target="tpu_custom_call" | custom-call | tf_op jit(solution)/shard_map/pallas_call | solution.py:421

commit v5 on v4

--- a/solution.py
+++ b/solution.py
@@ -156,6 +156,16 @@
     node_swap((1, 0, 0))
     loads[1].wait()
     lane = iota((nj, 128), 1)
+    def pack(i, acc):
+        for m in range(3):
+            at = m * ni + i
+            acc = jnp.where(lane == at, pltpu.roll(u[m, i, :, 0:128], at, 1), acc)
+        return acc
+
+    zs[...] = lax.fori_loop(0, ni, pack, jnp.zeros((nj, 128), F32), unroll=4)
+    for step in NODE_STEPS:
+        if step[2]:
+            node_swap(step)
     yd[...] = jnp.zeros(yd.shape, F32)
     for m in range(3):
         for i in range(ni):
@@ -163,17 +173,6 @@
         yd[m : m + 1, :] = u[m, 0, 0:1, :]
     node_swap((0, 1, 0))
     node_swap((1, 1, 0))
-
-    def pack(i, acc):
-        for m in range(3):
-            at = m * ni + i
-            acc = jnp.where(lane == at, pltpu.roll(u[m, i, :, 0:128], at, 1), acc)
-        return acc
-
-    zs[...] = lax.fori_loop(0, ni, pack, jnp.zeros((nj, 128), F32))
-    for step in NODE_STEPS:
-        if step[2]:
-            node_swap(step)
     loads[0].wait()
     high, low = band_weights(stiff[...])
     weights[0:192, :] = high
@@ -246,9 +245,9 @@
         * line_sum(me["gz"] * nk + iota((nj, nk), 1), nz * nk)
     )
     arrive(beside)
-    lax.fori_loop(0, ni, own_second, 0)
+    lax.fori_loop(0, ni, own_second, 0, unroll=2)
     arrive(below)
-    lax.fori_loop(0, ni, own_edges, 0)
+    lax.fori_loop(0, ni, own_edges, 0, unroll=2)
     arrive(far)
     for m in range(3):
         first_half(m, ni, rx[m])
@@ -306,7 +305,13 @@
             total = total + sums[base + at]
         return total
 
-    partial = jnp.concatenate([c_sum[:, :128] + c_sum[:, 128:], v_sum[:, :128] + v_sum[:, 128:]], 0)
+
+    def fold(x):
+        row = jnp.sum(x, axis=0, keepdims=True)
+        row = row[:, :128] + row[:, 128:]
+        return row + pltpu.roll(row, 64, 1)
+
+    partial = jnp.where(iota((1, 128), 1) < 64, fold(c_sum), fold(v_sum))
     x_sums = share(0, me["gx"], partial, line)
     arrive(x_copies)
 
@@ -323,7 +328,7 @@
         return lo, hi
 
     none = jnp.zeros((nj, 128), F32)
-    lo, hi = lax.fori_loop(0, ni, smooth_x, (none, none))
+    lo, hi = lax.fori_loop(0, ni, smooth_x, (none, none), unroll=4)
     zslo[...] = lo
     zshi[...] = hi
     side_copies = []
@@ -356,7 +361,7 @@
         out[i] = smooth_rows(wy, i)
         return carry
 
-    lax.fori_loop(0, ni, smooth_y, 0)
+    lax.fori_loop(0, ni, smooth_y, 0, unroll=4)
     totals[...] = gather(n["gx"], all_sums)
     for copies in (beside, below, far, x_copies, side_copies):
         finish(copies)
@@ -364,8 +369,10 @@
 
 def last_pass(cells, field, packs, totals, out, comp, vol):
     ni, nj, nk = field.shape
-    comp[0, 0] = jnp.sum(totals[0:8]) / cells
-    vol[0, 0] = jnp.sum(totals[8:16]) / cells
+    both = totals[...]
+    first = iota((1, 128), 1) < 64
+    comp[0, 0] = jnp.sum(jnp.where(first, both, 0.0)) / cells
+    vol[0, 0] = jnp.sum(jnp.where(first, 0.0, both)) / cells
     lanes = iota((nj, nk), 1)
 
     def twice(x):
@@ -381,7 +388,7 @@
         out[i] = 3.0 * t + 2.0 * (a1 + b1) + (a2 + b2)
         return carry
 
-    lax.fori_loop(0, ni, smooth_z, 0)
+    lax.fori_loop(0, ni, smooth_z, 0, unroll=4)
 
 
 def on_device(sizes, displacement, density, stiffness):
@@ -398,14 +405,14 @@
     later = [
         (ni + 4, nj, nk), (ni, nj + 16, nk),
         (2, ni, nk), (2, ni, nk), (2, ni, nk), (2, ni, nk),
-        (nj, 128), (nj, 128), (2, nj + 16, 128), (members, 16, 128),
+        (nj, 128), (nj, 128), (2, nj + 16, 128), (members, 1, 128),
     ]
     field, packs, totals = pl.pallas_call(
         functools.partial(kernel, sizes),
         out_shape=(
             jax.ShapeDtypeStruct((ni, nj, nk), F32),
             jax.ShapeDtypeStruct((2, nj, 128), F32),
-            jax.ShapeDtypeStruct((16, 128), F32),
+            jax.ShapeDtypeStruct((1, 128), F32),
         ),
         in_specs=[hbm] * 3,
         out_specs=(vmem, vmem, vmem),

time: 28.5 us -> 25.8 us (0.905)
  Pallas kernels: 27.8 us -> 25 us
    pallas_call x1, Pallas kernels: 24.9 us -> 23 us  [on_device(): pl.pallas_call(functools.partial(kernel, sizes), out_shape=(jax.ShapeDtyp...]
    pallas_call x1, Pallas kernels: 2.85 us -> 2.02 us  [on_device(): pl.pallas_call(functools.partial(last_pass, cells), out_shape=(jax.ShapeD...]
where the time goes in v5:
time: 25.8 us; the launch traced here: 25.6 us
  Pallas kernels  25 us (97%)
  between operations  0.64 us (2%)
    pallas_call x1, Pallas kernels, on_device(): pl.pallas_call(functools.partial(kernel, sizes), out_shape=(jax.ShapeDtyp...  23 us
    pallas_call x1, Pallas kernels, on_device(): pl.pallas_call(functools.partial(last_pass, cells), out_shape=(jax.ShapeD...  2.02 us

profile of v5, /device:TPU:0, one launch (start us, length us, event | category | flops | bytes accessed | tf_op | source)
XLA Modules:
  0.0 25.6 jit_solution(9167640272630797115)
XLA Ops:
  0.6 23.0 %shard_map.58 = (f32[16,32,256]{2,1,0:T(8,128)S(1)}, f32[2,32,128]{2,1,0:T(8,128)S(1)}, f32[1,128]{1,0:T(1,128)S(1)}) custom-call(f32[3,16,32,256]{3,2,1,0:T(8,128)} %u_hbm.1, f32[16,32,256]{2,1,0:T(8,128)} %rho_hbm.1, f32[24,24]{1,0:T(8,128)} %stiff_hbm.1), custom_call_target="tpu_custom_call" | custom-call | tf_op jit(solution)/shard_map/pallas_call | solution.py:410
  23.6 2.0 %shard_map.59 = (f32[16,32,256]{2,1,0:T(8,128)}, f32[1,1]{1,0:T(1,128)}, f32[1,1]{1,0:T(1,128)}) custom-call(f32[16,32,256]{2,1,0:T(8,128)S(1)} %get-tuple-element.9.field, f32[2,32,128]{2,1,0:T(8,128)S(1)} %get-tuple-element.10.packs, f32[1,128]{1,0:T(1,128)S(1)} %get-tuple-element.11.totals), custom_call_target="tpu_custom_call" | custom-call | tf_op jit(solution)/shard_map/pallas_call | solution.py:428
